TPU v7x, 32 devices: a whole 2x2x4 slice. The times are simulated.
32 devices in a mesh: gx: 4 (over x, core), gy: 4 (over z), gz: 2 (over y).
Axes of the slice: x: 2, y: 2, z: 4, core: 2. Of those that a mesh axis runs over, the one named last changes fastest.
Arguments:
- embeds: bfloat16 [256, 128, 2048], P(('gx', 'gy', 'gz')), may hold values from -6 to 6
- dest_device: int32 [256], P(('gx', 'gy', 'gz')), may hold values from 0 to 31, as said below
- shuffle_key: int32 [256], P(('gx', 'gy', 'gz')), may hold values from 0 to 255, each once
- lengths: int32 [8], replicated, may hold values from 1 to 4096
- gain: float32 [2048], replicated, may hold values from 0.1 to 1.9
Outputs:
- packed: bfloat16 [512, 128, 2048], P(('gx', 'gy', 'gz'))
Inputs may be any that keep to these rules, and one draw needn't show every extreme that they name: `dest_device`: device numbers are ((gx * 4) + gy) * 2 + gz. A device receives at most 16 tiles, and in every draw some devices receive exactly 16. The 2 devices sharing gx and gy send at most one tile to any one device and exactly 8 tiles to the devices of each gz index. Of one device's tiles at most 4 go to devices of one gz index, and some device reaches that.
All inputs are finite; a program needn't handle non-finite values.
Results may differ from a plain program's by a relative error of at most 0.001.
Values may be sent and summed in bfloat16 or wider, within the bound.
A program may use at most 128 MiB of HBM per device.

v0:
```python
import functools

import jax
import jax.numpy as jnp
from jax import lax
from jax.experimental import pallas as pl
from jax.experimental.pallas import tpu as pltpu
from jax.sharding import PartitionSpec as P

TILES_SEQ = 32
MESH = pl.DeviceIdType.MESH


def exchange_kernel(
    sizes, small_in, x_ref, gain_ref, recv_ref, keys_ref,
    small_ref, gain, small_sem, first_table, limit_table, note_out, notes, note_table, second, keys_out,
    x_sem, gain_sem, y_send, y_recv, g_send, g_recv, own_sem,
    note_send, note_recv, note_sem, key_send, key_recv, *buffers,
):
    nx, ny, depth, per_peer, chunk_rows = sizes
    chunks = len(chunk_rows)
    starts = [sum(chunk_rows[:c]) for c in range(chunks)]
    groups = nx * ny
    tiles_here, tile_rows, _ = x_ref.shape
    raw, first, arrived, outgoing = (buffers[i * chunks : (i + 1) * chunks] for i in range(4))
    gx, gy, gz = lax.axis_index("gx"), lax.axis_index("gy"), lax.axis_index("gz")
    group = gx * ny + gy
    me = group * depth + gz
    offsets = [(dx, dy) for dy in sorted(range(ny), key=lambda d: abs(d - ny // 2)) for dx in range(nx)]
    offsets.remove((0, 0))

    def load(c):
        return pltpu.make_async_copy(
            x_ref.at[:, pl.ds(starts[c], chunk_rows[c])], raw[c], x_sem.at[c]
        )

    def fill_tables():
        depths = [lax.rem(small_ref[0, i], depth) for i in range(tiles_here)]
        dest_groups = [lax.div(small_ref[0, i], depth) for i in range(tiles_here)]
        places, limits = [], []
        for i in range(tiles_here):
            spot = jnp.int32(0)
            for j in range(i):
                spot = spot + jnp.where(depths[j] == depths[i], 1, 0)
            places.append(depths[i] * per_peer + spot)
            tile = me * tiles_here + i
            length = small_ref[0, 2 * tiles_here + tile // TILES_SEQ]
            limits.append(jnp.maximum(length - tile % TILES_SEQ * tile_rows, 0))
        lane = lax.broadcasted_iota(jnp.int32, note_out.shape[1:], 1)
        for z in range(depth):
            row = jnp.zeros(note_out.shape[1:], jnp.int32)
            for p in range(per_peer):
                slot = z * per_peer + p
                tile, limit, dest_group, key = (jnp.int32(v) for v in (0, 0, -1, 0))
                for i in range(tiles_here):
                    hit = places[i] == slot
                    tile = jnp.where(hit, i, tile)
                    limit = jnp.where(hit, limits[i], limit)
                    dest_group = jnp.where(hit, dest_groups[i], dest_group)
                    key = jnp.where(hit, small_ref[0, tiles_here + i] + 1, key)
                first_table[slot] = tile
                limit_table[slot] = limit
                row = jnp.where(lane == p, dest_group, row)
                row = jnp.where(lane == per_peer + p, key, row)
            note_out[z] = row

    def normed(c, slot):
        rows = chunk_rows[c]
        values = raw[c][first_table[slot]].astype(jnp.float32)
        meansq = jnp.mean(values * values, axis=-1, keepdims=True)
        scaled = values * lax.rsqrt(jnp.maximum(meansq, 0.25)) * gain[...]
        row = starts[c] + lax.broadcasted_iota(jnp.int32, (rows, 1), 0)
        return jnp.where(row < limit_table[slot], scaled, 0.0).astype(jnp.bfloat16)

    def y_copy(c, dz, peer, origin):
        return pltpu.make_async_remote_copy(
            src_ref=first[c].at[dz - 1],
            dst_ref=arrived[c].at[pl.ds(origin * per_peer, per_peer)],
            send_sem=y_send.at[c, dz - 1],
            recv_sem=y_recv.at[c, dz - 1],
            device_id=(gx, gy, peer),
            device_id_type=MESH,
        )

    def peer_of(k):
        dx, dy = offsets[k]
        return lax.rem(gx + dx, nx), lax.rem(gy + dy, ny)

    def g_copy(c, k, px, py, origin):
        return pltpu.make_async_remote_copy(
            src_ref=outgoing[c].at[k],
            dst_ref=recv_ref.at[origin, pl.ds(starts[c], chunk_rows[c])],
            send_sem=g_send.at[c, k],
            recv_sem=g_recv.at[c, k],
            device_id=(px, py, gz),
            device_id_type=MESH,
        )

    def own_copy(c):
        return pltpu.make_async_copy(
            outgoing[c].at[groups - 1],
            recv_ref.at[group, pl.ds(starts[c], chunk_rows[c])],
            own_sem.at[c],
        )

    def note_copy(dz, peer, place):
        return pltpu.make_async_remote_copy(
            src_ref=note_out.at[peer],
            dst_ref=notes.at[place],
            send_sem=note_send.at[dz - 1],
            recv_sem=note_recv.at[dz - 1],
            device_id=(gx, gy, peer),
            device_id_type=MESH,
        )

    def key_copy(k, px, py, place):
        return pltpu.make_async_remote_copy(
            src_ref=keys_out.at[k],
            dst_ref=keys_ref.at[place],
            send_sem=key_send.at[k],
            recv_sem=key_recv.at[k],
            device_id=(px, py, gz),
            device_id_type=MESH,
        )

    def prepare(c):
        load(c).wait()
        for dz in range(1, depth):
            peer = lax.rem(gz + dz, depth)
            for p in range(per_peer):
                first[c][dz - 1, p] = normed(c, peer * per_peer + p)
        for p in range(per_peer):
            arrived[c][gz * per_peer + p] = normed(c, gz * per_peer + p)

    def send_first(c):
        for dz in range(1, depth):
            y_copy(c, dz, lax.rem(gz + dz, depth), gz).start()

    def find_slots():
        for dz in range(1, depth):
            origin = lax.rem(gz + depth - dz, depth)
            note_copy(dz, origin, origin).wait()
        tables = [
            pltpu.make_async_copy(
                notes.at[lax.rem(gz + dz, depth)], note_table.at[lax.rem(gz + dz, depth)], note_sem.at[dz]
            )
            for dz in range(1, depth)
        ]
        tables.append(pltpu.make_async_copy(note_out.at[gz], note_table.at[gz], note_sem.at[0]))
        for copy in tables:
            copy.start()
        for copy in tables:
            copy.wait()

        for k in range(groups):
            px, py = peer_of(k) if k < groups - 1 else (gx, gy)
            wanted = px * ny + py
            slot, key = jnp.int32(0), jnp.int32(0)
            for z in range(depth):
                for p in range(per_peer):
                    hit = note_table[z, 0, p] == wanted
                    slot = jnp.where(hit, z * per_peer + p, slot)
                    key = jnp.where(hit, note_table[z, 0, per_peer + p], key)
            second[k] = slot
            row = jnp.full(keys_out.shape[1:], key, jnp.int32)
            if k < groups - 1:
                keys_out[k] = row
            else:
                keys_ref[group] = row

    def forward(c):
        for dz in range(1, depth):
            origin = lax.rem(gz + depth - dz, depth)
            y_copy(c, dz, origin, origin).wait_recv()
        for k in range(groups):
            outgoing[c][k] = arrived[c][second[k]]
        for k in range(groups - 1):
            px, py = peer_of(k)
            g_copy(c, k, px, py, group).start()
        own_copy(c).start()

    small = [
        pltpu.make_async_copy(small_in, small_ref, small_sem),
        pltpu.make_async_copy(gain_ref, gain, gain_sem),
    ]
    for copy in small:
        copy.start()
    for c in range(chunks):
        load(c).start()
    barrier = pltpu.get_barrier_semaphore()
    for dz in range(1, depth):
        pl.semaphore_signal(
            barrier, inc=1, device_id=(gx, gy, lax.rem(gz + dz, depth)), device_id_type=MESH
        )
    for k in range(groups - 1):
        px, py = peer_of(k)
        pl.semaphore_signal(barrier, inc=1, device_id=(px, py, gz), device_id_type=MESH)
    for copy in small:
        copy.wait()
    fill_tables()
    prepare(0)
    pl.semaphore_wait(barrier, depth - 1 + groups - 1)
    for dz in range(1, depth):
        note_copy(dz, lax.rem(gz + dz, depth), gz).start()
    send_first(0)
    if chunks > 1:
        prepare(1)
        send_first(1)
    find_slots()
    forward(0)
    for k in range(groups - 1):
        px, py = peer_of(k)
        key_copy(k, px, py, group).start()
    for c in range(2, chunks):
        prepare(c)
        send_first(c)
        forward(c - 1)
    if chunks > 1:
        forward(chunks - 1)

    for c in range(chunks):
        for dz in range(1, depth):
            y_copy(c, dz, lax.rem(gz + dz, depth), gz).wait_send()
    sources = []
    for dx, dy in offsets:
        sources.append((lax.rem(gx + nx - dx, nx), lax.rem(gy + ny - dy, ny)))
    for k, (sx, sy) in enumerate(sources):
        key_copy(k, sx, sy, sx * ny + sy).wait()
    for c in range(chunks):
        for k, (sx, sy) in enumerate(sources):
            g_copy(c, k, sx, sy, sx * ny + sy).wait()
        own_copy(c).wait()


def place_kernel(source_ref, filled_ref, blocks_ref, out_ref, zeros, out_sem):
    cap = out_ref.shape[0]

    def store(slot):
        return pltpu.make_async_copy(blocks_ref.at[source_ref[slot]], out_ref.at[slot], out_sem.at[slot])

    for slot in range(cap):
        pl.when(filled_ref[slot] == 1)(lambda slot=slot: store(slot).start())
    zeros[...] = jnp.zeros_like(zeros)
    for slot in range(cap):

        @pl.when(filled_ref[slot] == 0)
        def _():
            pltpu.make_async_copy(zeros, out_ref.at[slot], out_sem.at[slot]).start()

    for slot in range(cap):
        store(slot).wait()


def shards(embeds, dest_device, shuffle_key, lengths, gain):
    tiles_here, tile_rows, width = embeds.shape
    nx, ny, depth = lax.axis_size("gx"), lax.axis_size("gy"), lax.axis_size("gz")
    groups = nx * ny
    per_peer = (tiles_here + depth - 1) // depth
    slots = depth * per_peer
    chunk_rows = (tile_rows,)
    if tile_rows % 128 == 0:
        chunk_rows = tuple(part * tile_rows // 16 for part in (1, 1, 2, 2, 4, 4, 2))
    chunks = len(chunk_rows)

    smem = pl.BlockSpec(memory_space=pltpu.SMEM)
    vmem = pl.BlockSpec(memory_space=pltpu.VMEM)
    hbm = pl.BlockSpec(memory_space=pl.ANY)
    lanes = -(-2 * per_peer // 128) * 128
    small = jnp.concatenate([dest_device, shuffle_key, lengths])
    small = jnp.pad(small, (0, -small.shape[0] % 128))[None, :]
    received, key_rows = pl.pallas_call(
        functools.partial(exchange_kernel, (nx, ny, depth, per_peer, chunk_rows)),
        out_shape=(
            jax.ShapeDtypeStruct((groups, tile_rows, width), jnp.bfloat16),
            jax.ShapeDtypeStruct((groups, 1, 128), jnp.int32),
        ),
        in_specs=[hbm] * 3,
        out_specs=(hbm, vmem),
        scratch_shapes=[
            pltpu.SMEM(small.shape, jnp.int32),
            pltpu.VMEM((1, width), jnp.float32),
            pltpu.SemaphoreType.DMA,
            pltpu.SMEM((slots,), jnp.int32),
            pltpu.SMEM((slots,), jnp.int32),
            pltpu.VMEM((depth, 1, lanes), jnp.int32),
            pltpu.VMEM((depth, 1, lanes), jnp.int32),
            pltpu.SMEM((depth, 1, lanes), jnp.int32),
            pltpu.SMEM((groups,), jnp.int32),
            pltpu.VMEM((groups, 1, 128), jnp.int32),
            pltpu.SemaphoreType.DMA((chunks,)),
            pltpu.SemaphoreType.DMA,
            pltpu.SemaphoreType.DMA((chunks, depth - 1)),
            pltpu.SemaphoreType.DMA((chunks, depth - 1)),
            pltpu.SemaphoreType.DMA((chunks, groups)),
            pltpu.SemaphoreType.DMA((chunks, groups)),
            pltpu.SemaphoreType.DMA((chunks,)),
            pltpu.SemaphoreType.DMA((depth,)),
            pltpu.SemaphoreType.DMA((depth,)),
            pltpu.SemaphoreType.DMA((depth,)),
            pltpu.SemaphoreType.DMA((groups,)),
            pltpu.SemaphoreType.DMA((groups,)),
        ]
        + [pltpu.VMEM((tiles_here, rows, width), jnp.bfloat16) for rows in chunk_rows]
        + [pltpu.VMEM((depth - 1, per_peer, rows, width), jnp.bfloat16) for rows in chunk_rows]
        + [pltpu.VMEM((slots, rows, width), jnp.bfloat16) for rows in chunk_rows]
        + [pltpu.VMEM((groups, rows, width), jnp.bfloat16) for rows in chunk_rows],
        compiler_params=pltpu.CompilerParams(
            collective_id=0, has_side_effects=True, vmem_limit_bytes=36 * 1024 * 1024
        ),
        name="exchange",
    )(small, embeds, gain.reshape(1, width))

    key_of = key_rows[:, 0, 0]
    valid = key_of > 0
    rank = jnp.sum((valid[None, :] & (key_of[None, :] < key_of[:, None])).astype(jnp.int32), axis=1)
    cap = 2 * tiles_here
    at = valid[None, :] & (rank[None, :] == jnp.arange(cap, dtype=jnp.int32)[:, None])
    source = jnp.sum(jnp.where(at, jnp.arange(groups, dtype=jnp.int32)[None, :], 0), axis=1).astype(jnp.int32)
    filled = jnp.sum(at.astype(jnp.int32), axis=1).astype(jnp.int32)

    return pl.pallas_call(
        place_kernel,
        out_shape=jax.ShapeDtypeStruct((cap, tile_rows, width), jnp.bfloat16),
        in_specs=[smem, smem, vmem],
        out_specs=hbm,
        scratch_shapes=[
            pltpu.VMEM((tile_rows, width), jnp.bfloat16),
            pltpu.SemaphoreType.DMA((cap,)),
        ],
        compiler_params=pltpu.CompilerParams(vmem_limit_bytes=24 * 1024 * 1024),
        name="place",
    )(source, filled, received)


def solution(mesh):
    return jax.shard_map(
        shards,
        mesh=mesh,
        in_specs=(
            P(("gx", "gy", "gz"), None, None),
            P(("gx", "gy", "gz")),
            P(("gx", "gy", "gz")),
            P(),
            P(),
        ),
        out_specs=P(("gx", "gy", "gz"), None, None),
        check_vma=False,
    )
```

profile of v0, /device:TPU:1, one launch (start us, length us, event | category | flops | bytes accessed | tf_op | source)
XLA Modules:
  0.0 197.5 jit_solution(12787704376812360420)
XLA Ops:
  0.0 0.8 pad_add_fusion
  0.8 0.0 copy-start
  0.8 2.2 %copy-done = bf16[8,128,2048]{2,1,0:T(8,128)(2,1)S(1)} copy-done((bf16[8,128,2048]{2,1,0:T(8,128)(2,1)S(1)}, bf16[8,128,2048]{2,1,0:T(8,128)(2,1)}, u32[]{:S(2)}) %copy-start) | copy-done | bytes 4194328
  3.0 0.0 copy-start.1
  3.0 0.7 copy-done.1
  3.7 189.1 %exchange.1 = (bf16[16,128,2048]{2,1,0:T(8,128)(2,1)S(1)}, s32[16,1,128]{2,1,0:T(1,128)S(1)}) custom-call(s32[1,128]{1,0:T(1,128)S(1)} %pad_bitcast_fusion.small_in, bf16[8,128,2048]{2,1,0:T(8,128)(2,1)S(1)} %copy-done, f32[1,2048]{1,0:T(1,128)S(1)} %bitcast.3), custom_call_target="tpu_custom_call" | custom-call | tf_op jit(solution)/shard_map/exchange/pallas_call | solution.py:271
  192.8 0.4 slice_reduce_fusion
  193.2 0.2 convert_reduce_fusion.1
  193.4 0.1 convert_reduce_fusion
  193.5 4.0 %place.1 = bf16[16,128,2048]{2,1,0:T(8,128)(2,1)} custom-call(s32[16]{0:T(128)S(1)} %get-tuple-element.10.source_ref, s32[16]{0:T(128)S(1)} %get-tuple-element.9.filled_ref, bf16[16,128,2048]{2,1,0:T(8,128)(2,1)S(1)} %get-tuple-element.8.blocks_ref), custom_call_target="tpu_custom_call" | custom-call | tf_op jit(solution)/shard_map/place/pallas_call | solution.py:321
  (2 shorter events, 0.0 us)
Async XLA Ops:
  0.8 2.2 %copy-start = (bf16[8,128,2048]{2,1,0:T(8,128)(2,1)S(1)}, bf16[8,128,2048]{2,1,0:T(8,128)(2,1)}, u32[]{:S(2)}) copy-start(bf16[8,128,2048]{2,1,0:T(8,128)(2,1)} %x_ref.1) | copy-start | bytes 12582916
  3.0 0.7 copy-start.1
where the time goes:
time: 201 us; the launch traced here: 197 us
  Pallas kernels  193 us (96%)
  local copies, waits for them, and re-layouts  3.27 us (2%)
    pallas_call x1, Pallas kernels, shards(): pl.pallas_call(functools.partial(exchange_kernel, (nx, ny, depth, per_pee...  189 us

commit v1 on v0

--- a/solution.py
+++ b/solution.py
@@ -8,6 +8,8 @@
 from jax.sharding import PartitionSpec as P
 
 TILES_SEQ = 32
+CLASSES = (10, 12, 16)
+CHUNKS = (1, 1, 2, 2, 2, 2, 2, 2, 1, 1)
 MESH = pl.DeviceIdType.MESH
 
 
@@ -251,7 +253,7 @@
         store(slot).wait()
 
 
-def shards(embeds, dest_device, shuffle_key, lengths, gain):
+def direct(embeds, dest_device, shuffle_key, lengths, gain):
     tiles_here, tile_rows, width = embeds.shape
     nx, ny, depth = lax.axis_size("gx"), lax.axis_size("gy"), lax.axis_size("gz")
     groups = nx * ny
@@ -332,6 +334,434 @@
     )(source, filled, received)
 
 
+def table_kernel(sizes, mine_ref, table_ref, send, recv):
+    nx, ny, depth = sizes
+    devices = nx * ny * depth
+    me = (lax.axis_index("gx") * ny + lax.axis_index("gy")) * depth + lax.axis_index("gz")
+
+    def place_of(device):
+        return lax.div(device, ny * depth), lax.rem(lax.div(device, depth), ny), lax.rem(device, depth)
+
+    def row_copy(step, target, row):
+        return pltpu.make_async_remote_copy(
+            src_ref=mine_ref,
+            dst_ref=table_ref.at[row],
+            send_sem=send.at[step - 1],
+            recv_sem=recv.at[step - 1],
+            device_id=place_of(target),
+            device_id_type=MESH,
+        )
+
+    barrier = pltpu.get_barrier_semaphore()
+    for step in range(1, devices):
+        pl.semaphore_signal(
+            barrier, inc=1, device_id=place_of(lax.rem(me + step, devices)), device_id_type=MESH
+        )
+    table_ref[me] = mine_ref[...]
+    pl.semaphore_wait(barrier, devices - 1)
+    for step in range(1, devices):
+        row_copy(step, lax.rem(me + step, devices), me).start()
+    for step in range(1, devices):
+        source = lax.rem(me + devices - step, devices)
+        row_copy(step, source, source).wait()
+
+
+def line_kernel(
+    sizes, plan_ref, x_ref, gain_ref, out_ref,
+    plan, gain, plan_sem, gain_sem, x_sem, y_send, y_recv, a_send, a_recv, b_send, b_recv,
+    g_send, g_recv, out_sem, *buffers,
+):
+    nx, ny, depth, per_peer, chunk_rows, near, far, back, at = sizes
+    chunks = len(chunk_rows)
+    starts = [sum(chunk_rows[:c]) for c in range(chunks)]
+    half = ny // 2
+    slots = depth * per_peer
+    cap = out_ref.shape[0]
+    raw, first, pool, inflow, inward, outward, outgoing, received, staged = (
+        buffers[i * chunks : (i + 1) * chunks] for i in range(9)
+    )
+    gx, gy, gz = lax.axis_index("gx"), lax.axis_index("gy"), lax.axis_index("gz")
+    low = gy < half
+    level = jnp.where(low, gy, ny - 1 - gy)
+    inner = jnp.where(low, gy + 1, gy - 1)
+    outer = jnp.clip(jnp.where(low, gy - 1, gy + 1), 0, ny - 1)
+    middle = level == half - 1
+
+    def load(c):
+        return pltpu.make_async_copy(
+            x_ref.at[:, pl.ds(starts[c], chunk_rows[c])], raw[c], x_sem.at[c]
+        )
+
+    def normed(c, slot):
+        rows = chunk_rows[c]
+        values = raw[c][plan[0, at["tile"] + slot]].astype(jnp.float32)
+        meansq = jnp.mean(values * values, axis=-1, keepdims=True)
+        scaled = values * lax.rsqrt(jnp.maximum(meansq, 0.25)) * gain[...]
+        row = starts[c] + lax.broadcasted_iota(jnp.int32, (rows, 1), 0)
+        return jnp.where(row < plan[0, at["limit"] + slot], scaled, 0.0).astype(jnp.bfloat16)
+
+    def y_copy(c, dz, peer, origin):
+        return pltpu.make_async_remote_copy(
+            src_ref=first[c].at[dz - 1],
+            dst_ref=pool[c].at[pl.ds(origin * per_peer, per_peer)],
+            send_sem=y_send.at[c, dz - 1],
+            recv_sem=y_recv.at[c, dz - 1],
+            device_id=(gx, gy, peer),
+            device_id_type=MESH,
+        )
+
+    def near_copy(c, peer):
+        return pltpu.make_async_remote_copy(
+            src_ref=inward[c].at[pl.ds(0, near)],
+            dst_ref=pool[c].at[pl.ds(slots, near)],
+            send_sem=a_send.at[c],
+            recv_sem=a_recv.at[c],
+            device_id=(gx, peer, gz),
+            device_id_type=MESH,
+        )
+
+    def cross_copy(c, peer):
+        return pltpu.make_async_remote_copy(
+            src_ref=inward[c],
+            dst_ref=inflow[c],
+            send_sem=a_send.at[c],
+            recv_sem=b_recv.at[c],
+            device_id=(gx, peer, gz),
+            device_id_type=MESH,
+        )
+
+    def back_copy(c, peer):
+        return pltpu.make_async_remote_copy(
+            src_ref=outward[c],
+            dst_ref=inflow[c].at[pl.ds(0, back)],
+            send_sem=b_send.at[c],
+            recv_sem=b_recv.at[c],
+            device_id=(gx, peer, gz),
+            device_id_type=MESH,
+        )
+
+    def g_copy(c, dx, peer, origin):
+        return pltpu.make_async_remote_copy(
+            src_ref=outgoing[c].at[dx - 1],
+            dst_ref=received[c].at[pl.ds(origin * ny, ny)],
+            send_sem=g_send.at[c, dx - 1],
+            recv_sem=g_recv.at[c, dx - 1],
+            device_id=(peer, gy, gz),
+            device_id_type=MESH,
+        )
+
+    def out_copy(c):
+        return pltpu.make_async_copy(
+            staged[c], out_ref.at[:, pl.ds(starts[c], chunk_rows[c])], out_sem.at[c]
+        )
+
+    def prepare(c):
+        load(c).wait()
+        for dz in range(1, depth):
+            peer = lax.rem(gz + dz, depth)
+            for p in range(per_peer):
+                first[c][dz - 1, p] = normed(c, peer * per_peer + p)
+        for dz in range(1, depth):
+            y_copy(c, dz, lax.rem(gz + dz, depth), gz).start()
+        for p in range(per_peer):
+            pool[c][gz * per_peer + p] = normed(c, gz * per_peer + p)
+
+    def either(c, code):
+        held = pool[c][jnp.clip(code, 0, slots + near - 1)]
+        came = inflow[c][jnp.clip(code - slots - near, 0, far - 1)]
+        return jnp.where(code < slots + near, held, came)
+
+    def send_inward(c):
+        for dz in range(1, depth):
+            origin = lax.rem(gz + depth - dz, depth)
+            y_copy(c, dz, origin, origin).wait_recv()
+
+        @pl.when(level > 0)
+        def _():
+            near_copy(c, outer).wait_recv()
+
+        @pl.loop(0, far)
+        def _(p):
+            inward[c][p] = pool[c][plan[0, at["inward"] + p]]
+
+        @pl.when(middle)
+        def _():
+            cross_copy(c, inner).start()
+
+        @pl.when(jnp.logical_not(middle))
+        def _():
+            near_copy(c, inner).start()
+
+    def deliver(c):
+        @pl.when(middle)
+        def _():
+            cross_copy(c, inner).wait_recv()
+
+        @pl.when(jnp.logical_not(middle))
+        def _():
+            back_copy(c, inner).wait_recv()
+
+        @pl.when(level > 0)
+        def _():
+            @pl.loop(0, back)
+            def _(p):
+                outward[c][p] = either(c, plan[0, at["outward"] + p])
+
+            back_copy(c, outer).start()
+
+        for dx in range(1, nx):
+            peer = lax.rem(gx + dx, nx)
+
+            @pl.loop(0, ny)
+            def _(k):
+                outgoing[c][dx - 1, k] = either(c, plan[0, at["deliver"] + peer * ny + k])
+
+        for dx in range(1, nx):
+            g_copy(c, dx, lax.rem(gx + dx, nx), gx).start()
+
+        @pl.loop(0, ny)
+        def _(k):
+            received[c][gx * ny + k] = either(c, plan[0, at["deliver"] + gx * ny + k])
+
+    def place(c):
+        for dx in range(1, nx):
+            origin = lax.rem(gx + nx - dx, nx)
+            g_copy(c, dx, origin, origin).wait_recv()
+
+        @pl.loop(0, cap)
+        def _(slot):
+            source = plan[0, at["place"] + slot]
+            found = received[c][jnp.maximum(source, 0)]
+            staged[c][slot] = jnp.where(source >= 0, found, jnp.zeros_like(found))
+
+        out_copy(c).start()
+
+    small = [
+        pltpu.make_async_copy(plan_ref, plan, plan_sem),
+        pltpu.make_async_copy(gain_ref, gain, gain_sem),
+    ]
+    for copy in small:
+        copy.start()
+    for c in range(chunks):
+        load(c).start()
+    barrier = pltpu.get_barrier_semaphore()
+    for dz in range(1, depth):
+        pl.semaphore_signal(
+            barrier, inc=1, device_id=(gx, gy, lax.rem(gz + dz, depth)), device_id_type=MESH
+        )
+    for dx in range(1, nx):
+        pl.semaphore_signal(
+            barrier, inc=1, device_id=(lax.rem(gx + dx, nx), gy, gz), device_id_type=MESH
+        )
+    pl.semaphore_signal(barrier, inc=1, device_id=(gx, inner, gz), device_id_type=MESH)
+
+    @pl.when(level > 0)
+    def _():
+        pl.semaphore_signal(barrier, inc=1, device_id=(gx, outer, gz), device_id_type=MESH)
+
+    for copy in small:
+        copy.wait()
+    pl.semaphore_wait(barrier, depth - 1 + nx - 1 + 1 + jnp.where(level > 0, 1, 0))
+
+    ahead = 4
+    for step in range(chunks + ahead + 2):
+        if step < chunks:
+            prepare(step)
+        if 0 <= step - 1 < chunks:
+            send_inward(step - 1)
+        if 0 <= step - 1 - ahead < chunks:
+            deliver(step - 1 - ahead)
+        if 0 <= step - 2 - ahead < chunks:
+            place(step - 2 - ahead)
+
+    for c in range(chunks):
+        for dz in range(1, depth):
+            y_copy(c, dz, lax.rem(gz + dz, depth), gz).wait_send()
+
+        @pl.when(middle)
+        def _():
+            cross_copy(c, inner).wait_send()
+
+        @pl.when(jnp.logical_not(middle))
+        def _():
+            near_copy(c, inner).wait_send()
+
+        @pl.when(level > 0)
+        def _():
+            back_copy(c, outer).wait_send()
+
+        for dx in range(1, nx):
+            g_copy(c, dx, lax.rem(gx + dx, nx), gx).wait_send()
+        out_copy(c).wait()
+
+
+def count(mask):
+    return jnp.sum(mask.astype(jnp.int32), axis=1)
+
+
+def pick(value, mask, position, wanted):
+    hit = mask[None, :] & (position[None, :] == jnp.arange(wanted, dtype=jnp.int32)[:, None])
+    return jnp.sum(jnp.where(hit, value[None, :], 0), axis=1)
+
+
+def shards(embeds, dest_device, shuffle_key, lengths, gain):
+    tiles_here, tile_rows, width = embeds.shape
+    nx, ny, depth = lax.axis_size("gx"), lax.axis_size("gy"), lax.axis_size("gz")
+    devices = nx * ny * depth
+    per_peer = (tiles_here + depth - 1) // depth
+    slots = depth * per_peer
+    half = ny // 2
+    cap = 2 * tiles_here
+    if ny % 2 or tile_rows % 128 or slots > tiles_here:
+        return direct(embeds, dest_device, shuffle_key, lengths, gain)
+
+    most = half * min(tiles_here, nx * half)
+    near_most = max([(e + 1) * min(tiles_here, nx * (ny - 1 - e)) for e in range(half - 1)] + [1])
+    back_most = max([(ny - e) * min(tiles_here, nx * e) for e in range(1, half)] + [1])
+    classes = sorted({max(1, most * part // 16) for part in CLASSES})
+
+    lanes = -(-2 * tiles_here // 128) * 128
+    mine = jnp.pad(jnp.concatenate([dest_device, shuffle_key]), (0, lanes - 2 * tiles_here))[None, :]
+    vmem = pl.BlockSpec(memory_space=pltpu.VMEM)
+    table = pl.pallas_call(
+        functools.partial(table_kernel, (nx, ny, depth)),
+        out_shape=jax.ShapeDtypeStruct((devices, 1, lanes), jnp.int32),
+        in_specs=[vmem],
+        out_specs=vmem,
+        scratch_shapes=[pltpu.SemaphoreType.DMA((devices - 1,))] * 2,
+        compiler_params=pltpu.CompilerParams(collective_id=0, has_side_effects=True),
+        name="tables",
+    )(mine)
+
+    gx, gy, gz = lax.axis_index("gx"), lax.axis_index("gy"), lax.axis_index("gz")
+    group = gx * ny + gy
+    me = group * depth + gz
+    dest = table[:, 0, :tiles_here].reshape(-1)
+    keys = table[:, 0, tiles_here : 2 * tiles_here].reshape(-1)
+    order = jnp.arange(devices * tiles_here, dtype=jnp.int32)
+    before = order[None, :] < order[:, None]
+    source = order // tiles_here
+    from_x, from_y = source // (ny * depth), source // depth % ny
+    to_x, to_y, to_z = dest // (ny * depth), dest // depth % ny, dest % depth
+
+    bounds = jnp.arange(ny - 1, dtype=jnp.int32)
+    lane = from_x * depth + to_z
+    hop_up = (from_y[None, :] <= bounds[:, None]) & (to_y[None, :] > bounds[:, None])
+    hop_down = (from_y[None, :] > bounds[:, None]) & (to_y[None, :] <= bounds[:, None])
+    hops = jnp.concatenate([hop_up, hop_down])
+    in_lane = lane[None, :] == jnp.arange(nx * depth, dtype=jnp.int32)[:, None]
+    load = jnp.max(jnp.sum((hops[:, None, :] & in_lane[None, :, :]).astype(jnp.int32), axis=2))
+
+    low = gy < half
+    level = jnp.where(low, gy, ny - 1 - gy)
+    depth_from = jnp.where(low, from_y, ny - 1 - from_y)
+    depth_to = jnp.where(low, to_y, ny - 1 - to_y)
+    in_my_lane = (from_x == gx) & (to_z == gz)
+    inward = in_my_lane & (depth_from <= level) & (depth_to > level)
+    near_in = in_my_lane & (depth_from < level) & (depth_to >= level)
+    outward = in_my_lane & (depth_from >= level) & (depth_to < level)
+    far_in = in_my_lane & (depth_from > level) & (depth_to <= level)
+    landing = in_my_lane & (depth_to == level)
+    to_me = dest == me
+
+    same_source = source[:, None] == source[None, :]
+    spot = count(before & same_source & (to_z[:, None] == to_z[None, :]))
+    at_inward = count(before & inward[None, :])
+    at_near = count(before & near_in[None, :])
+    at_outward = count(before & outward[None, :])
+    at_far = count(before & far_in[None, :])
+    at_landing = count(before & (landing[None, :] & (to_x[:, None] == to_x[None, :])))
+    at_me = count(before & (to_me[None, :] & (from_x[:, None] == from_x[None, :])))
+    rank = count((keys[None, :] < keys[:, None]) & to_me[None, :])
+    own_slot = source % depth * per_peer + spot
+
+    def plan_for(far):
+        near, back = min(far, near_most), min(far, back_most)
+        code = jnp.where(
+            depth_from == level,
+            own_slot,
+            jnp.where(depth_from < level, slots + at_near, slots + near + at_far),
+        )
+        tile = me * tiles_here + jnp.arange(tiles_here, dtype=jnp.int32)
+        length = lengths[tile // TILES_SEQ]
+        limit = jnp.maximum(length - tile % TILES_SEQ * tile_rows, 0)
+        here = dest_device % depth
+        early = jnp.arange(tiles_here)[None, :] < jnp.arange(tiles_here)[:, None]
+        my_slot = here * per_peer + count(early & (here[:, None] == here[None, :]))
+        always = jnp.ones((tiles_here,), jnp.bool_)
+        parts = {
+            "tile": pick(jnp.arange(tiles_here, dtype=jnp.int32), always, my_slot, slots),
+            "limit": pick(limit, always, my_slot, slots),
+            "inward": pick(code, inward, at_inward, far),
+            "outward": pick(code, outward, at_outward, back),
+            "deliver": pick(code, landing, to_x * ny + at_landing, nx * ny),
+            "place": pick(from_x * ny + at_me + 1, to_me, rank, cap) - 1,
+        }
+        at, total = {}, 0
+        for name, part in parts.items():
+            at[name] = total
+            total += part.shape[0]
+        joined = jnp.concatenate(list(parts.values()))
+        return jnp.pad(joined, (0, -total % 128))[None, :], at, near, back
+
+    chunk_rows = tuple(part * tile_rows // 16 for part in CHUNKS)
+    chunks = len(chunk_rows)
+    hbm = pl.BlockSpec(memory_space=pl.ANY)
+
+    def branch(index, far):
+        def run(embeds, gain):
+            plan, at, near, back = plan_for(far)
+            counts = (
+                (tiles_here,),
+                (depth - 1, per_peer),
+                (slots + near,),
+                (far,),
+                (far,),
+                (back,),
+                (nx - 1, ny),
+                (nx * ny,),
+                (cap,),
+            )
+            return pl.pallas_call(
+                functools.partial(
+                    line_kernel, (nx, ny, depth, per_peer, chunk_rows, near, far, back, at)
+                ),
+                out_shape=jax.ShapeDtypeStruct((cap, tile_rows, width), jnp.bfloat16),
+                in_specs=[hbm] * 3,
+                out_specs=hbm,
+                scratch_shapes=[
+                    pltpu.SMEM(plan.shape, jnp.int32),
+                    pltpu.VMEM((1, width), jnp.float32),
+                    pltpu.SemaphoreType.DMA,
+                    pltpu.SemaphoreType.DMA,
+                    pltpu.SemaphoreType.DMA((chunks,)),
+                    pltpu.SemaphoreType.DMA((chunks, depth - 1)),
+                    pltpu.SemaphoreType.DMA((chunks, depth - 1)),
+                    pltpu.SemaphoreType.DMA((chunks,)),
+                    pltpu.SemaphoreType.DMA((chunks,)),
+                    pltpu.SemaphoreType.DMA((chunks,)),
+                    pltpu.SemaphoreType.DMA((chunks,)),
+                    pltpu.SemaphoreType.DMA((chunks, nx - 1)),
+                    pltpu.SemaphoreType.DMA((chunks, nx - 1)),
+                    pltpu.SemaphoreType.DMA((chunks,)),
+                ]
+                + [pltpu.VMEM((*lead, rows, width), jnp.bfloat16) for lead in counts for rows in chunk_rows],
+                compiler_params=pltpu.CompilerParams(
+                    collective_id=1 + index, has_side_effects=True, vmem_limit_bytes=60 * 1024 * 1024
+                ),
+                name=f"line{far}",
+            )(plan, embeds, gain)
+
+        return run
+
+    chosen = jnp.int32(0)
+    for bound in classes[:-1]:
+        chosen = chosen + (load > bound).astype(jnp.int32)
+    return lax.switch(
+        chosen, [branch(i, far) for i, far in enumerate(classes)], embeds, gain.reshape(1, width)
+    )
+
+
 def solution(mesh):
     return jax.shard_map(
         shards,

time: 201 us -> 254 us (1.26); the launches traced: 197 us -> 253 us
  Pallas kernels: 193 us -> 234 us
  local copies, waits for them, and re-layouts: 3.27 us -> 12 us
  other arithmetic: 1.08 us -> 5.02 us
    pallas_call x2, Pallas kernels: 193 us -> 234 us  [the longest x1 224 us: run(): pl.pallas_call(functools.partial(line_kernel, (nx, ny, depth, per_peer, c...]
    unnamed x4 -> x1, local copies, waits for them, and re-layouts: 2.89 us -> 8.44 us
where the time goes in v1:
time: 254 us; the launch traced here: 253 us
  Pallas kernels  234 us (92%)
  local copies, waits for them, and re-layouts  12 us (5%)
  other arithmetic  5.02 us (2%)
    pallas_call x1, Pallas kernels, run(): pl.pallas_call(functools.partial(line_kernel, (nx, ny, depth, per_peer, c...  224 us
    pallas_call x1, Pallas kernels, shards(): pl.pallas_call(functools.partial(table_kernel, (nx, ny, depth)), out_shap...  10.5 us
    unnamed x1, local copies, waits for them, and re-layouts  8.44 us

profile of v1, /device:TPU:1, one launch (start us, length us, event | category | flops | bytes accessed | tf_op | source)
XLA Modules:
  0.0 253.2 jit_solution(17942223804458460021)
XLA Ops:
  0.0 0.7 pad_add_fusion.1
  0.7 0.5 pad_bitcast_fusion.3.mine_ref
  1.3 10.5 %tables.1 = s32[32,1,128]{2,1,0:T(1,128)} custom-call(s32[1,128]{1,0:T(1,128)} %pad_bitcast_fusion.3.mine_ref), custom_call_target="tpu_custom_call" | custom-call | tf_op jit(solution)/shard_map/tables/pallas_call | solution.py:626
  11.8 0.9 slice_reduce_fusion
  12.8 0.1 lt.251
  12.9 0.1 reshape_squeeze.3
  13.1 0.2 convert_reduce_fusion.3
  13.3 0.7 reduce_max.9
  15.4 0.2 fusion.48
  15.6 0.1 fusion.53
  15.8 229.0 %conditional.1 = (bf16[16,128,2048]{2,1,0:T(8,128)(2,1)}) conditional(s32[]{:T(128)} %clamp.3, (s32[8]{0:T(128)}, s32[]{:T(128)}, s32[8]{0:T(128)}, pred[256]{0:T(512)(128)(4,1)S(1)}, s32[256,256]{1,0:T(8,128)S(1)}, /*index=5*/s32[]{:T(128)}, s32[256]{0:T(256)S(1)}, s32[256]{0:T(256)S(1)}, pred[256]{0:T(512)(128)(4,1)S(1)}, ...), branch_computations={%region_2.18_spmd, %region_18.34_spmd, %region_34.50_spmd} | conditional | flops 590093 | bytes 2134656 | solution.py:760
  15.8 0.7 and_select_fusion.7
  16.5 0.2 convert_reduce_fusion.1
  16.7 0.1 reduce_sum.391
  16.8 0.1 reduce_sum.392
  16.9 0.1 reduce_sum.393
  17.0 0.1 reduce_sum.394
  17.2 0.1 reduce_sum.396
  17.3 0.1 select_reduce_fusion.8
  17.4 0.1 reduce_sum.398
  17.5 0.1 reduce_sum.400
  17.7 0.1 reduce_sum.401
  17.8 0.1 select_reduce_fusion.6
  17.9 1.3 gather_fusion.1
  19.2 0.7 fusion.25
  19.9 0.1 select_reduce_fusion.10
  20.1 0.1 concatenate.14
  20.1 0.5 pad_bitcast_fusion.1.plan_ref
  20.7 223.7 %line12.2 = bf16[16,128,2048]{2,1,0:T(8,128)(2,1)} custom-call(s32[1,128]{1,0:T(1,128)} %pad_bitcast_fusion.1.plan_ref, bf16[8,128,2048]{2,1,0:T(8,128)(2,1)} %get-tuple-element.480.x_ref, f32[1,2048]{1,0:T(1,128)} %bitcast.18), custom_call_target="tpu_custom_call" | custom-call | tf_op jit(solution)/shard_map/cond/branch_1_fun/line12/pallas_call | solution.py:725
  244.8 8.4 %copy.13 = bf16[16,128,2048]{2,1,0:T(8,128)(2,1)} copy(bf16[16,128,2048]{2,1,0:T(8,128)(2,1)} %get-tuple-element.507) | data formatting | bytes 16777216
  (22 shorter events, 0.3 us)
